TPU v7x, 32 devices: a whole 2x2x4 slice. The times are simulated.
32 devices in a mesh: level: 4 (over x, core), body: 8 (over z, y).
Axes of the slice: x: 2, y: 2, z: 4, core: 2. Of those that a mesh axis runs over, the one named last changes fastest.
Arguments:
- state: float32 [4, 6, 8192], P('level', None, 'body'), may hold values from -14 to 14
- history: float32 [4, 3, 6, 8192], P('level', None, None, 'body'), may hold values from -6 to 6
- masses: float32 [8192], P('body'), may hold values from 0.25 to 4
Outputs:
- final_state: float32 [4, 6, 8192], P('level', None, 'body')
All inputs are finite; a program needn't handle non-finite values.
Results may differ from a plain program's by a relative error of at most 0.0001.
Values sent between devices are 32-bit elements; how exact they have to be, the bound alone decides.
No kernel may reach another device: no remote copies, remote signals or barrier semaphores. Data moves between devices by JAX's collectives and lax.ppermute only.
A program may use at most 64 MiB of HBM per device.

v0:
```python
import jax
import jax.numpy as jnp
from jax import lax
from jax.experimental import pallas as pl
from jax.experimental.pallas import tpu as pltpu
from jax.sharding import PartitionSpec as P

SOFTEN = 0.05
DELTA = 0.05
COUPLING = 512.0

F32, BF16 = jnp.float32, jnp.bfloat16
TILE = 256
PIECE = 32
LANES = 128
HALF = TILE // PIECE // 2


def split3(x):
    first = x.astype(BF16).astype(F32)
    rest = x - first
    second = rest.astype(BF16).astype(F32)
    return first, second, rest - second


def pull_kernel(own_count, blocks, row, own_ref, src_ref, mu_ref, out_ref, s_ref, p_ref, t_ref, w_ref):
    passes = own_count // (2 * TILE)
    chunks = blocks * own_count // TILE
    pieces = TILE // PIECE
    units = range(2)

    def main(*accs):
        accs = list(accs)
        d_acc = [[[accs.pop(0) for _ in range(pieces)] for _ in range(2)] for _ in units]
        o_acc = [[[accs.pop(0) for _ in range(2)] for _ in range(passes)] for _ in units]

        own = own_ref[...]
        square = jnp.sum(own * own, axis=0, keepdims=True)
        zero8 = jnp.zeros((8, own_count), F32)
        target = jnp.concatenate([own, jnp.ones((1, own_count), F32), square, zero8[0:3]], axis=0)
        stack = list(split3(target)) * 3
        stack = stack + [zero8] * (TILE // 8 - len(stack))
        t_ref[...] = jnp.concatenate(stack, axis=0).astype(BF16)

        def prepare(block, carry):
            pos = src_ref[block, row:row + 3, :]
            mu = mu_ref[block, 6:7, :]
            norm = jnp.sum(pos * pos, axis=0, keepdims=True)
            source = jnp.concatenate([-2.0 * mu * pos, mu * (norm + SOFTEN), mu, zero8[0:3]], axis=0)
            s1, s2, s3 = split3(source)
            p1, p2, p3 = split3(jnp.concatenate([pos, jnp.ones((1, own_count), F32), zero8[0:4]], axis=0))
            stacked = jnp.concatenate([s1] * 3 + [s2] * 3 + [s3] * 3 + [zero8] * 7, axis=0)
            start = pl.multiple_of(block * own_count, own_count)
            for lane in range(0, own_count, LANES):
                s_ref[pl.ds(start + lane, LANES), :] = stacked[:, lane:lane + LANES].T.astype(BF16)
            p_ref[0:16, pl.ds(start, own_count)] = jnp.concatenate([p1, p2], axis=0).astype(BF16)
            p_ref[16:32, pl.ds(start, own_count)] = jnp.concatenate([p3, zero8], axis=0).astype(BF16)
            return carry

        lax.fori_loop(0, blocks, prepare, 0)

        def push_targets(unit, which):
            low = (unit * passes + which) * TILE
            pltpu.matmul_push_rhs(t_ref[:, low:low + TILE], staging_register=0, mxu_index=unit)

        def distances(unit, slot, piece, chunk, latch):
            start = chunk * TILE + piece * PIECE
            if not isinstance(chunk, int):
                start = pl.multiple_of(start, PIECE)
            rows = jnp.concatenate([s_ref[pl.ds(start, PIECE), :], jnp.zeros((PIECE, LANES), BF16)], axis=1)
            pltpu.matmul_acc_lhs(d_acc[unit][slot][piece], rows, load_staged_rhs=0 if latch else None)

        def weigh(unit, slot, piece):
            inverse = lax.rsqrt(pltpu.matmul_pop(d_acc[unit][slot][piece]))
            weight = inverse * inverse * inverse
            high = weight.astype(BF16)
            low = (weight - high.astype(F32)).astype(BF16)
            w_ref[slot, unit, 0, piece * PIECE:(piece + 1) * PIECE, :] = high
            w_ref[slot, unit, 1, piece * PIECE:(piece + 1) * PIECE, :] = low

        def push_weights(unit, slot, part):
            pltpu.matmul_push_rhs(w_ref[slot, unit, part], staging_register=1, mxu_index=unit)

        def pull(unit, part, which, chunk):
            start = chunk * TILE
            if not isinstance(chunk, int):
                start = pl.multiple_of(start, TILE)
            rows = p_ref[0:16 if part else 32, pl.ds(start, TILE)]
            pltpu.matmul_acc_lhs(o_acc[unit][which][part], rows, load_staged_rhs=1)

        def step(slot, last, following, which):
            for part in range(2):
                if following is not None:
                    for unit in units:
                        push_targets(unit, which)
                if last is not None:
                    for unit in units:
                        push_weights(unit, 1 - slot, part)
                for piece in range(part * HALF, (part + 1) * HALF):
                    for unit in units:
                        weigh(unit, slot, piece)
                        if following is not None:
                            distances(unit, slot, piece, following, piece == part * HALF)
                if last is not None:
                    for unit in units:
                        pull(unit, part, *last)

        for unit in units:
            for acc in sum(d_acc[unit], []) + sum(o_acc[unit], []):
                pltpu.matmul_pop(acc)
            push_targets(unit, 0)
        for slot in range(2):
            for unit in units:
                for piece in range(pieces):
                    distances(unit, slot, piece, slot, slot == 0 and piece == 0)
        for which in range(passes):
            step(0, (which - 1, chunks - 1) if which else None, 2, which)
            step(1, (which, 0), 3, which)

            def pair(index, carry):
                step(0, (which, 2 * index - 1), 2 * index + 2, which)
                step(1, (which, 2 * index), 2 * index + 3, which)
                return carry

            lax.fori_loop(1, chunks // 2 - 1, pair, 0)
            more = which + 1 < passes
            step(0, (which, chunks - 3), 0 if more else None, which + 1)
            step(1, (which, chunks - 2), 1 if more else None, which + 1)
        for part in range(2):
            for unit in units:
                push_weights(unit, 1, part)
                pull(unit, part, passes - 1, chunks - 1)
        for unit in units:
            for which in range(passes):
                a = pltpu.matmul_pop(o_acc[unit][which][0])
                b = pltpu.matmul_pop(o_acc[unit][which][1])
                total = (a[0:8] + b[0:8]) + (a[8:16] + b[8:16]) + a[16:24]
                low = (unit * passes + which) * TILE
                pulled = total[0:3] - own_ref[:, low:low + TILE] * total[3:4]
                out_ref[:, low:low + TILE] = pulled * (COUPLING / (blocks * own_count))

    shapes = []
    for unit in units:
        shapes += [pltpu.ACC(unit)((PIECE, TILE), F32)] * (2 * pieces)
    for unit in units:
        shapes += [pltpu.ACC(unit)((32, TILE), F32), pltpu.ACC(unit)((16, TILE), F32)] * passes
    pl.run_scoped(main, *shapes)


def acceleration(own, sources, scales, row):
    own_count = own.shape[1]
    blocks = sources.shape[0]
    count = blocks * own_count
    whole = pl.BlockSpec(memory_space=pltpu.VMEM)

    def kernel(*refs):
        pull_kernel(own_count, blocks, row, *refs)

    return pl.pallas_call(
        kernel,
        out_shape=jax.ShapeDtypeStruct((3, own_count), F32),
        in_specs=[whole] * 3,
        out_specs=whole,
        scratch_shapes=[
            pltpu.VMEM((count, LANES), BF16),
            pltpu.VMEM((32, count), BF16),
            pltpu.VMEM((TILE, own_count), BF16),
            pltpu.VMEM((2, 2, 2, TILE, TILE), BF16),
        ],
        cost_estimate=pl.CostEstimate(
            flops=20 * own_count * count, bytes_accessed=32 * count, transcendentals=own_count * count
        ),
    )(own, sources, scales)


def everyone(rows, axis):
    copies = jnp.broadcast_to(rows[None], (lax.axis_size(axis),) + rows.shape)
    return lax.all_to_all(copies, axis, 0, 0)


def on_device(state, history, masses):
    level = lax.axis_index("level")
    above = level > 0
    p0, v0 = state[0, 0:3], state[0, 3:6]
    stored = jnp.where(above, history[0], 0.0)
    hp = [stored[k, 0:3] for k in range(3)]
    hv = [stored[k, 3:6] for k in range(3)]

    def lower(rows, gathered, distance):
        picked = lax.dynamic_index_in_dim(gathered, jnp.maximum(level - distance, 0), 0, False)
        return jnp.where(level >= distance, picked, 0.0)

    def advance(value, force, past, newest):
        old, older, oldest = past[2], past[1], past[0]
        return value + DELTA * (force - old) + DELTA * (
            oldest / 24.0 - 5.0 * older / 24.0 + 19.0 * old / 24.0 + 9.0 * newest / 24.0
        )

    w0 = lower(None, lax.all_gather(v0, "level"), 1)
    p1 = advance(p0, v0, hp, w0)
    scale = jnp.exp2(jnp.log2(masses) * (-2.0 / 3.0))[None]
    first = everyone(jnp.concatenate([p0, p1, scale, scale], axis=0), "body")
    a0 = acceleration(p0, first, first, 0)
    a1 = acceleration(p1, first, first, 3)

    zero = jnp.zeros_like(v0)
    x1 = advance(v0, a0, hv, zero)
    x2 = advance(x1, a1, [hv[1], hv[2], zero], zero)
    gathered = lax.all_gather(jnp.concatenate([a0, a1, x1, x2], axis=0), "level")
    below = lower(None, gathered, 1)
    second = lower(None, gathered, 2)
    b0, b1 = below[0:3], below[3:6]
    w1 = below[6:9] + DELTA * (9.0 / 24.0) * second[0:3]
    w2 = below[9:12] + DELTA * ((4.0 / 24.0) * second[0:3] + (9.0 / 24.0) * second[3:6])
    v1 = advance(v0, a0, hv, b0)
    v2 = advance(v1, a1, [hv[1], hv[2], b0], b1)
    p2 = advance(p1, v1, [hp[1], hp[2], w0], w1)
    p3 = advance(p2, v2, [hp[2], w0, w1], w2)
    later = everyone(jnp.concatenate([p2, p3, p3[0:2]], axis=0), "body")
    a2 = acceleration(p2, later, first, 0)
    a3 = acceleration(p3, later, first, 3)

    x3 = advance(v2, a2, [hv[2], b0, b1], zero)
    gathered = lax.all_gather(jnp.concatenate([a2, a3, x3], axis=0), "level")
    below = lower(None, gathered, 1)
    second = lower(None, gathered, 2)
    b2, b3 = below[0:3], below[3:6]
    w3 = below[6:9] + DELTA * (9.0 / 24.0) * second[0:3]
    v3 = advance(v2, a2, [hv[2], b0, b1], b2)
    v4 = advance(v3, a3, [b0, b1, b2], b3)
    p4 = advance(p3, v3, [w0, w1, w2], w3)
    return jnp.concatenate([p4, v4], axis=0)[None]


def solution(mesh):
    placed = (P("level", None, "body"), P("level", None, None, "body"), P("body"))
    return jax.shard_map(
        on_device, mesh=mesh, in_specs=placed, out_specs=P("level", None, "body"), check_vma=False
    )
```

profile of v0, /device:TPU:0, one launch (start us, length us, event | category | flops | bytes accessed | tf_op | source)
XLA Modules:
  0.0 117.1 jit_solution(16939551246025808169)
XLA Ops:
  0.0 0.0 copy-start.12
  0.0 0.7 copy-done.12
  0.7 0.7 fusion.42
  1.4 0.0 copy-start.8
  1.4 0.0 copy-start.10
  1.5 6.2 %all_gather.15 = f32[4,3,1024]{2,1,0:T(4,128)S(1)} all-gather(f32[1,3,1024]{2,1,0:T(4,128)S(1)} %copy.13), channel_id=1, replica_groups=mesh['level'=4,'body'=8] {'level'}, dimensions={0}, use_global_device_ids=true | all-gather | bytes 61440 | tf_op jit(solution)/shard_map/all_gather | solution.py:199
  7.7 0.0 copy-done.8
  7.7 0.0 copy-start.3
  7.7 0.0 copy-done.10
  7.8 0.6 copy-done.3
  8.3 0.7 broadcast_in_dim.39
  9.0 6.4 %all-to-all-start = ((f32[8,8,1024]{2,1,0:T(8,128)}), f32[8,8,1024]{2,1,0:T(8,128)S(1)}, u32[]{:S(2)}, u32[]{:S(2)}) async-start(f32[8,8,1024]{2,1,0:T(8,128)} %broadcast_in_dim.39), calls=%async_computation | async-start | bytes 524288 | tf_op jit(solution)/shard_map/all_to_all | solution.py:178
  15.4 9.4 %all-to-all-done.refs_1_.refs_2_ = f32[8,8,1024]{2,1,0:T(8,128)S(1)} async-done(((f32[8,8,1024]{2,1,0:T(8,128)}), f32[8,8,1024]{2,1,0:T(8,128)S(1)}, u32[]{:S(2)}, u32[]{:S(2)}) %all-to-all-start) | async-done | bytes 262176 | tf_op jit(solution)/shard_map/all_to_all | solution.py:178
  24.8 0.0 copy-start
  24.8 0.7 copy-done
  25.5 15.3 %shard_map.37 = f32[3,1024]{1,0:T(4,128)} custom-call(f32[3,1024]{1,0:T(4,128)} %bitcast.211, f32[8,8,1024]{2,1,0:T(8,128)} %copy-done, f32[8,8,1024]{2,1,0:T(8,128)} %copy-done), custom_call_target="tpu_custom_call" | custom-call | flops 167772160 | bytes 262144 | tf_op jit(solution)/shard_map/pallas_call | solution.py:159
  40.8 0.0 copy-start.6
  40.8 15.3 %shard_map.38 = f32[3,1024]{1,0:T(4,128)} custom-call(f32[3,1024]{1,0:T(4,128)} %copy-done.3, f32[8,8,1024]{2,1,0:T(8,128)} %copy-done, f32[8,8,1024]{2,1,0:T(8,128)} %copy-done), custom_call_target="tpu_custom_call" | custom-call | flops 167772160 | bytes 262144 | tf_op jit(solution)/shard_map/pallas_call | solution.py:159
  56.1 0.0 copy-done.6
  56.1 0.0 copy-start.7
  56.1 0.8 multiply_add_fusion.6
  56.9 0.0 copy-done.7
  57.0 5.8 %all-gather.2 = f32[4,12,1024]{2,1,0:T(8,128)S(1)} all-gather(f32[1,12,1024]{2,1,0:T(8,128)S(1)} %maximum_bitcast_fusion), channel_id=2, replica_groups=mesh['level'=4,'body'=8] {'level'}, dimensions={0}, use_global_device_ids=true | all-gather | bytes 245760 | tf_op jit(solution)/shard_map/all_gather | solution.py:209
  62.7 0.0 copy-start.4
  62.8 0.7 copy-done.4
  63.5 0.1 fusion.36
  63.6 0.0 copy-start.1
  63.6 0.0 copy-start.11
  63.6 0.5 copy-done.1
  64.2 0.0 copy-done.11
  64.2 12.9 %all_to_all.10.refs_1_ = f32[8,8,1024]{2,1,0:T(8,128)} all-to-all(f32[8,8,1024]{2,1,0:T(8,128)S(1)} %broadcast_in_dim.41), channel_id=1, replica_groups=mesh['level'=4,'body'=8] {'body'}, dimensions={0} | all-to-all | bytes 524288 | tf_op jit(solution)/shard_map/all_to_all | solution.py:178
  77.1 15.3 %shard_map.39 = f32[3,1024]{1,0:T(4,128)} custom-call(f32[3,1024]{1,0:T(4,128)} %copy-done.11, f32[8,8,1024]{2,1,0:T(8,128)} %all_to_all.10.refs_1_, f32[8,8,1024]{2,1,0:T(8,128)} %copy-done), custom_call_target="tpu_custom_call" | custom-call | flops 167772160 | bytes 262144 | tf_op jit(solution)/shard_map/pallas_call | solution.py:159
  92.4 0.7 multiply_add_fusion.1
  93.1 0.0 copy-start.5
  93.1 15.3 %shard_map.40 = f32[3,1024]{1,0:T(4,128)} custom-call(f32[3,1024]{1,0:T(4,128)} %copy-done.1, f32[8,8,1024]{2,1,0:T(8,128)} %all_to_all.10.refs_1_, f32[8,8,1024]{2,1,0:T(8,128)} %copy-done), custom_call_target="tpu_custom_call" | custom-call | flops 167772160 | bytes 262144 | tf_op jit(solution)/shard_map/pallas_call | solution.py:159
  108.4 0.0 copy-done.5
  108.4 0.7 maximum_bitcast_fusion.1
  109.2 5.8 %all-gather.3 = f32[4,9,1024]{2,1,0:T(8,128)S(1)} all-gather(f32[1,9,1024]{2,1,0:T(8,128)S(1)} %maximum_bitcast_fusion.1), channel_id=3, replica_groups=mesh['level'=4,'body'=8] {'level'}, dimensions={0}, use_global_device_ids=true | all-gather | bytes 184320 | tf_op jit(solution)/shard_map/all_gather | solution.py:224
  115.0 0.0 copy-start.2
  115.0 0.7 copy-done.2
  115.7 0.0 copy-start.9
  115.7 0.1 fusion.11
  115.7 0.7 copy-done.9
  116.4 0.6 copy.11
  (14 shorter events, 0.2 us)
Async XLA Ops:
  0.0 0.7 copy-start.12
  1.4 6.2 %copy-start.8 = (f32[1,3,6,1024]{3,0,2,1:T(1,128)S(1)}, f32[1,3,6,1024]{3,0,2,1:T(1,128)}, u32[]{:S(2)}) copy-start(f32[1,3,6,1024]{3,0,2,1:T(1,128)} %param.4) | copy-start | bytes 221188
  1.4 6.3 %copy-start.10 = (f32[1,3,1024]{2,1,0:T(4,128)}, f32[1,3,1024]{2,1,0:T(4,128)S(1)}, u32[]{:S(2)}) copy-start(f32[1,3,1024]{2,1,0:T(4,128)S(1)} %copy.27) | copy-start | bytes 36868
  7.7 0.6 copy-start.3
  9.0 15.8 %all-to-all-start = ((f32[8,8,1024]{2,1,0:T(8,128)}), f32[8,8,1024]{2,1,0:T(8,128)S(1)}, u32[]{:S(2)}, u32[]{:S(2)}) async-start(f32[8,8,1024]{2,1,0:T(8,128)} %broadcast_in_dim.39), calls=%async_computation | async-start | bytes 524288 | tf_op jit(solution)/shard_map/all_to_all | solution.py:178
  24.8 0.7 copy-start
  40.8 15.3 %copy-start.6 = (f32[3,1024]{1,0:T(4,128)S(1)}, f32[3,1024]{1,0:T(4,128)}, u32[]{:S(2)}) copy-start(f32[3,1024]{1,0:T(4,128)} %shard_map.37) | copy-start | bytes 36868
  56.1 0.8 copy-start.7
  62.7 0.7 copy-start.4
  63.6 0.6 copy-start.1
  63.6 0.6 copy-start.11
  93.1 15.3 %copy-start.5 = (f32[3,1024]{1,0:T(4,128)S(1)}, f32[3,1024]{1,0:T(4,128)}, u32[]{:S(2)}) copy-start(f32[3,1024]{1,0:T(4,128)} %shard_map.39) | copy-start | bytes 36868
  115.0 0.7 copy-start.2
  115.7 0.7 copy-start.9
where the time goes:
time: 118 us; the launch traced here: 117 us
  Pallas kernels  61.1 us (52%)
  blocking collectives  30.7 us (26%)
  waiting for transfers between devices  9.43 us (8%)
  local copies, waits for them, and re-layouts  6.69 us (6%)
  starting transfers between devices  6.36 us (5%)
  other arithmetic  2.64 us (2%)
    pallas_call x4, Pallas kernels, acceleration(): pl.pallas_call(kernel, out_shape=jax.ShapeDtypeStruct((3, own_count), F32...  61.1 us
    all_to_all x1, blocking collectives, everyone(): return lax.all_to_all(copies, axis, 0, 0)  12.9 us
    all_to_all x1, waiting for transfers between devices, everyone(): return lax.all_to_all(copies, axis, 0, 0)  9.43 us
    all_to_all x1, starting transfers between devices, everyone(): return lax.all_to_all(copies, axis, 0, 0)  6.36 us
    all_gather x1, blocking collectives, on_device(): w0 = lower(None, lax.all_gather(v0, 'level'), 1)  6.19 us
    all_gather x1, blocking collectives, on_device(): lax.all_gather(jnp.concatenate([a0, a1, x1, x2], axis=0), 'level')  5.78 us
    all_gather x1, blocking collectives, on_device(): gathered = lax.all_gather(jnp.concatenate([a2, a3, x3], axis=0), 'level')  5.78 us
    unnamed x28, local copies, waits for them, and re-layouts  4.59 us
  transfers between devices with their start and end apart: 1, of which 1 were waited for; matrix products, arithmetic and copies ran while one was open for 0% of the time, Pallas kernels for 0%

commit v1 on v0

v1 whole, which is shorter than its diff:
```python
import jax
import jax.numpy as jnp
from jax import lax
from jax.experimental import pallas as pl
from jax.experimental.pallas import tpu as pltpu
from jax.sharding import PartitionSpec as P

SOFTEN = 0.05
DELTA = 0.05
COUPLING = 512.0
STEP = DELTA * 9.0 / 24.0

F32, BF16 = jnp.float32, jnp.bfloat16
TILE = 256
PIECE = 16
UNROLL = 4
LANES = 128


def split3(x):
    first = x.astype(BF16).astype(F32)
    rest = x - first
    second = rest.astype(BF16).astype(F32)
    return first, second, rest - second


def pull_kernel(own_count, blocks, row, own_ref, src_ref, mu_ref, out_ref, s_ref, p_ref, t_ref, w_ref):
    tiles = own_count // TILE
    chunks = blocks * own_count // TILE
    pieces = TILE // PIECE

    def main(*accs):
        accs = list(accs)
        d_acc = [[accs.pop(0) for _ in range(pieces)] for _ in range(2)]
        o_acc = [[accs.pop(0) for _ in range(2)] for _ in range(tiles)]

        own = own_ref[...]
        square = jnp.sum(own * own, axis=0, keepdims=True)
        zero8 = jnp.zeros((8, own_count), F32)
        one = jnp.ones((1, own_count), F32)
        t1, t2, t3 = split3(jnp.concatenate([own, one, square, zero8[0:3]], axis=0))
        t_ref[...] = jnp.concatenate([t1, t2, t3, t1, t2, t1] + [zero8] * (TILE // 8 - 6), axis=0)

        def prepare(block, carry):
            pos = src_ref[block, row:row + 3, :]
            mu = mu_ref[block, 6:7, :]
            norm = jnp.sum(pos * pos, axis=0, keepdims=True)
            s1, s2, s3 = split3(jnp.concatenate([-2.0 * mu * pos, mu * (norm + SOFTEN), mu, zero8[0:3]], axis=0))
            stacked = jnp.concatenate([s1, s1, s1, s2, s2, s3] + [zero8] * 10, axis=0)
            start = pl.multiple_of(block * own_count, own_count)
            for lane in range(0, own_count, LANES):
                s_ref[pl.ds(start + lane, LANES), :] = stacked[:, lane:lane + LANES].T
            p1, p2, p3 = split3(jnp.concatenate([pos, one, zero8[0:4]], axis=0))
            p_ref[:, pl.ds(start, own_count)] = jnp.concatenate([p1, p2, p3], axis=0)
            return carry

        lax.fori_loop(0, blocks, prepare, 0)

        def push_targets(tile):
            pltpu.matmul_push_rhs(t_ref[:, tile * TILE:(tile + 1) * TILE], staging_register=0, mxu_index=0)

        def distances(slot, piece, chunk, latch):
            start = chunk * TILE + piece * PIECE
            if not isinstance(chunk, int):
                start = pl.multiple_of(start, PIECE)
            rows = jnp.concatenate([s_ref[pl.ds(start, PIECE), :], jnp.zeros((PIECE, LANES), F32)], axis=1)
            pltpu.matmul_acc_lhs(d_acc[slot][piece], rows, load_staged_rhs=0 if latch else None)

        def weigh(slot, piece):
            inverse = lax.rsqrt(pltpu.matmul_pop(d_acc[slot][piece]))
            weight = inverse * inverse * inverse
            high = weight.astype(BF16).astype(F32)
            w_ref[slot, 0, piece * PIECE:(piece + 1) * PIECE, :] = high
            w_ref[slot, 1, piece * PIECE:(piece + 1) * PIECE, :] = weight - high

        def pull(slot, part, tile, chunk):
            start = chunk * TILE
            if not isinstance(chunk, int):
                start = pl.multiple_of(start, TILE)
            pltpu.matmul_push_rhs(w_ref[slot, part], staging_register=part, mxu_index=1)
            rows = p_ref[0:16 if part else 24, pl.ds(start, TILE)]
            pltpu.matmul_acc_lhs(o_acc[tile][part], rows, load_staged_rhs=part)

        def step(slot, last, following, new_tile=None):
            if new_tile is not None:
                push_targets(new_tile)
            for piece in range(pieces):
                if last is not None and piece % (pieces // 2) == 0:
                    pull(1 - slot, piece // (pieces // 2), *last)
                weigh(slot, piece)
                if following is not None:
                    distances(slot, piece, following, new_tile is not None and piece == 0)

        for acc in d_acc[0] + d_acc[1] + sum(o_acc, []):
            pltpu.matmul_pop(acc)
        push_targets(0)
        for slot in range(2):
            for piece in range(pieces):
                distances(slot, piece, slot, slot + piece == 0)
        for tile in range(tiles):
            step(0, (tile - 1, chunks - 1) if tile else None, 2)
            step(1, (tile, 0), 3)
            spare = (chunks - 4) % UNROLL

            def middle(first, steps):
                for index in range(steps):
                    step(index % 2, (tile, first + index - 1), first + index + 2)

            def group(index, carry):
                middle(2 + spare + index * UNROLL, UNROLL)
                return carry

            middle(2, spare)
            lax.fori_loop(0, (chunks - 4) // UNROLL, group, 0)
            more = tile + 1 < tiles
            step(0, (tile, chunks - 3), 0 if more else None, tile + 1 if more else None)
            step(1, (tile, chunks - 2), 1 if more else None)
        for part in range(2):
            pull(1, part, tiles - 1, chunks - 1)
        for tile in range(tiles):
            a = pltpu.matmul_pop(o_acc[tile][0])
            b = pltpu.matmul_pop(o_acc[tile][1])
            total = (a[0:8] + b[0:8]) + (a[8:16] + b[8:16]) + a[16:24]
            low = tile * TILE
            pulled = total[0:3] - own_ref[:, low:low + TILE] * total[3:4]
            out_ref[:, low:low + TILE] = pulled * (COUPLING / (blocks * own_count))

    shapes = [pltpu.ACC(0)((PIECE, TILE), F32)] * (2 * pieces)
    shapes += [pltpu.ACC(1)((24, TILE), F32), pltpu.ACC(1)((16, TILE), F32)] * tiles
    pl.run_scoped(main, *shapes)


def acceleration(own, sources, scales, row):
    own_count = own.shape[1]
    blocks = sources.shape[0]
    count = blocks * own_count
    whole = pl.BlockSpec(memory_space=pltpu.VMEM)

    def kernel(*refs):
        pull_kernel(own_count, blocks, row, *refs)

    return pl.pallas_call(
        kernel,
        out_shape=pltpu.VMEM((3, own_count), F32),
        in_specs=[whole] * 3,
        out_specs=whole,
        scratch_shapes=[
            pltpu.VMEM((count, LANES), F32),
            pltpu.VMEM((24, count), F32),
            pltpu.VMEM((TILE, own_count), F32),
            pltpu.VMEM((2, 2, TILE, TILE), F32),
        ],
        cost_estimate=pl.CostEstimate(
            flops=6 * TILE * own_count * count, bytes_accessed=32 * count, transcendentals=own_count * count
        ),
    )(*(pltpu.with_memory_space_constraint(x, pltpu.VMEM) for x in (own, sources, scales)))


def everyone(rows, axis):
    copies = jnp.broadcast_to(rows[None], (lax.axis_size(axis),) + rows.shape)
    return lax.all_to_all(copies, axis, 0, 0)


def on_device(state, history, masses):
    level = lax.axis_index("level")
    above = level > 0
    p0, v0 = state[0, 0:3], state[0, 3:6]
    stored = jnp.where(above, history[0], 0.0)
    hp = [stored[k, 0:3] for k in range(3)]
    hv = [stored[k, 3:6] for k in range(3)]

    def lower(gathered, distance):
        picked = lax.dynamic_index_in_dim(gathered, jnp.maximum(level - distance, 0), 0, False)
        return jnp.where(level >= distance, picked, 0.0)

    def advance(value, force, past, newest):
        old, older, oldest = past[2], past[1], past[0]
        return value + DELTA * (force - old) + DELTA * (
            oldest / 24.0 - 5.0 * older / 24.0 + 19.0 * old / 24.0 + 9.0 * newest / 24.0
        )

    w0 = lower(lax.all_gather(v0, "level"), 1)
    p1 = advance(p0, v0, hp, w0)
    scale = jnp.exp2(jnp.log2(masses) * (-2.0 / 3.0))[None]
    first = everyone(jnp.concatenate([p0, p1, scale, scale], axis=0), "body")
    a0 = acceleration(p0, first, first, 0)
    a1 = acceleration(p1, first, first, 3)

    zero = jnp.zeros_like(v0)
    x1 = advance(v0, a0, hv, zero)
    x2 = advance(x1, a1, [hv[1], hv[2], zero], zero)
    gathered = lax.all_gather(jnp.concatenate([a0, a1, x1, x2], axis=0), "level")
    below = lower(gathered, 1)
    second = lower(gathered, 2)
    b0, b1 = below[0:3], below[3:6]
    w1 = below[6:9] + DELTA * (9.0 / 24.0) * second[0:3]
    w2 = below[9:12] + DELTA * ((4.0 / 24.0) * second[0:3] + (9.0 / 24.0) * second[3:6])
    v1 = advance(v0, a0, hv, b0)
    v2 = advance(v1, a1, [hv[1], hv[2], b0], b1)
    p2 = advance(p1, v1, [hp[1], hp[2], w0], w1)
    p3 = advance(p2, v2, [hp[2], w0, w1], w2)
    later = everyone(jnp.concatenate([p2, p3, p3[0:2]], axis=0), "body")
    a2 = acceleration(p2, later, first, 0)
    a3 = acceleration(p3, later, first, 3)

    x3 = advance(v2, a2, [hv[2], b0, b1], zero)
    gathered = lax.all_gather(jnp.concatenate([a2, a3, x3], axis=0), "level")
    below = lower(gathered, 1)
    second = lower(gathered, 2)
    b2, b3 = below[0:3], below[3:6]
    w3 = below[6:9] + DELTA * (9.0 / 24.0) * second[0:3]
    v3 = advance(v2, a2, [hv[2], b0, b1], b2)
    v4 = advance(v3, a3, [b0, b1, b2], b3)
    p4 = advance(p3, v3, [w0, w1, w2], w3)
    return jnp.concatenate([p4, v4], axis=0)[None]


def solution(mesh):
    placed = (P("level", None, "body"), P("level", None, None, "body"), P("body"))
    return jax.shard_map(
        on_device, mesh=mesh, in_specs=placed, out_specs=P("level", None, "body"), check_vma=False
    )
```

time: 118 us -> 95.4 us (0.81)
  Pallas kernels: 61.1 us -> 45.3 us
  local copies, waits for them, and re-layouts: 6.69 us -> 2.81 us
  other arithmetic: 2.64 us -> 0.43 us
    pallas_call x4, Pallas kernels: 61.1 us -> 45.3 us  [acceleration(): pl.pallas_call(kernel, out_shape=pltpu.VMEM((3, own_count), F32), in_spec...]
    unnamed x28 -> x6, local copies, waits for them, and re-layouts: 4.59 us -> 0.7 us
    add x6, other arithmetic: 1.77 us -> 0.27 us  [advance(): value + DELTA * (force - old)]
where the time goes in v1:
time: 95.4 us; the launch traced here: 95 us
  Pallas kernels  45.3 us (47%)
  blocking collectives  30.6 us (32%)
  waiting for transfers between devices  9.43 us (10%)
  starting transfers between devices  6.36 us (7%)
  local copies, waits for them, and re-layouts  2.81 us (3%)
    pallas_call x4, Pallas kernels, acceleration(): pl.pallas_call(kernel, out_shape=pltpu.VMEM((3, own_count), F32), in_spec...  45.3 us
    all_to_all x1, blocking collectives, everyone(): return lax.all_to_all(copies, axis, 0, 0)  12.8 us
    all_to_all x1, waiting for transfers between devices, everyone(): return lax.all_to_all(copies, axis, 0, 0)  9.43 us
    all_to_all x1, starting transfers between devices, everyone(): return lax.all_to_all(copies, axis, 0, 0)  6.36 us
    all_gather x1, blocking collectives, on_device(): w0 = lower(lax.all_gather(v0, 'level'), 1)  6.19 us
    all_gather x1, blocking collectives, on_device(): lax.all_gather(jnp.concatenate([a0, a1, x1, x2], axis=0), 'level')  5.78 us
    all_gather x1, blocking collectives, on_device(): gathered = lax.all_gather(jnp.concatenate([a2, a3, x3], axis=0), 'level')  5.78 us
  transfers between devices with their start and end apart: 1, of which 1 were waited for; matrix products, arithmetic and copies ran while one was open for 0% of the time, Pallas kernels for 0%

profile of v1, /device:TPU:0, one launch (start us, length us, event | category | flops | bytes accessed | tf_op | source)
XLA Modules:
  0.0 95.0 jit_solution(4745780362444684645)
XLA Ops:
  0.0 0.0 copy-start.1
  0.0 0.7 copy-done.1
  0.7 0.7 fusion.42
  1.4 0.0 copy-start
  1.5 6.2 %all_gather.15 = f32[4,3,1024]{2,1,0:T(4,128)S(1)} all-gather(f32[1,3,1024]{2,1,0:T(4,128)S(1)} %copy.13), channel_id=1, replica_groups=mesh['level'=4,'body'=8] {'level'}, dimensions={0}, use_global_device_ids=true | all-gather | bytes 61440 | tf_op jit(solution)/shard_map/all_gather | solution.py:182
  7.6 0.0 copy-done
  7.7 0.7 broadcast_in_dim.39
  8.5 6.4 %all-to-all-start = ((f32[8,8,1024]{2,1,0:T(8,128)}), f32[8,8,1024]{2,1,0:T(8,128)S(1)}, u32[]{:S(2)}, u32[]{:S(2)}) async-start(f32[8,8,1024]{2,1,0:T(8,128)} %broadcast_in_dim.39), calls=%async_computation | async-start | bytes 524288 | tf_op jit(solution)/shard_map/all_to_all | solution.py:161
  14.8 9.4 %all-to-all-done.refs_1_.refs_2_ = f32[8,8,1024]{2,1,0:T(8,128)S(1)} async-done(((f32[8,8,1024]{2,1,0:T(8,128)}), f32[8,8,1024]{2,1,0:T(8,128)S(1)}, u32[]{:S(2)}, u32[]{:S(2)}) %all-to-all-start) | async-done | bytes 262176 | tf_op jit(solution)/shard_map/all_to_all | solution.py:161
  24.2 11.3 %shard_map.37 = f32[3,1024]{1,0:T(4,128)S(1)} custom-call(f32[3,1024]{1,0:T(4,128)S(1)} %bitcast.211, f32[8,8,1024]{2,1,0:T(8,128)S(1)} %all-to-all-done.refs_1_.refs_2_, f32[8,8,1024]{2,1,0:T(8,128)S(1)} %all-to-all-done.refs_1_.refs_2_), custom_call_target="tpu_custom_call" | custom-call | flops 12884901888 | bytes 262144 | tf_op jit(solution)/shard_map/pallas_call | solution.py:142
  35.6 11.3 %shard_map.38 = f32[3,1024]{1,0:T(4,128)S(1)} custom-call(f32[3,1024]{1,0:T(4,128)S(1)} %fusion.25.refs_0_, f32[8,8,1024]{2,1,0:T(8,128)S(1)} %all-to-all-done.refs_1_.refs_2_, f32[8,8,1024]{2,1,0:T(8,128)S(1)} %all-to-all-done.refs_1_.refs_2_), custom_call_target="tpu_custom_call" | custom-call | flops 12884901888 | bytes 262144 | tf_op jit(solution)/shard_map/pallas_call | solution.py:142
  47.0 5.8 %all-gather.2 = f32[4,12,1024]{2,1,0:T(8,128)S(1)} all-gather(f32[1,12,1024]{2,1,0:T(8,128)S(1)} %maximum_bitcast_fusion), channel_id=2, replica_groups=mesh['level'=4,'body'=8] {'level'}, dimensions={0}, use_global_device_ids=true | all-gather | bytes 245760 | tf_op jit(solution)/shard_map/all_gather | solution.py:192
  52.8 0.1 fusion.36
  52.9 12.8 %all_to_all.10.refs_1_ = f32[8,8,1024]{2,1,0:T(8,128)S(1)} all-to-all(f32[8,8,1024]{2,1,0:T(8,128)S(1)} %broadcast_in_dim.41), channel_id=1, replica_groups=mesh['level'=4,'body'=8] {'body'}, dimensions={0} | all-to-all | bytes 524288 | tf_op jit(solution)/shard_map/all_to_all | solution.py:161
  65.7 11.3 %shard_map.39 = f32[3,1024]{1,0:T(4,128)S(1)} custom-call(f32[3,1024]{1,0:T(4,128)S(1)} %get-tuple-element.8.refs_0_, f32[8,8,1024]{2,1,0:T(8,128)S(1)} %all_to_all.10.refs_1_, f32[8,8,1024]{2,1,0:T(8,128)S(1)} %all-to-all-done.refs_1_.refs_2_), custom_call_target="tpu_custom_call" | custom-call | flops 12884901888 | bytes 262144 | tf_op jit(solution)/shard_map/pallas_call | solution.py:142
  77.1 11.3 %shard_map.40 = f32[3,1024]{1,0:T(4,128)S(1)} custom-call(f32[3,1024]{1,0:T(4,128)S(1)} %get-tuple-element.7.refs_0_, f32[8,8,1024]{2,1,0:T(8,128)S(1)} %all_to_all.10.refs_1_, f32[8,8,1024]{2,1,0:T(8,128)S(1)} %all-to-all-done.refs_1_.refs_2_), custom_call_target="tpu_custom_call" | custom-call | flops 12884901888 | bytes 262144 | tf_op jit(solution)/shard_map/pallas_call | solution.py:142
  88.5 5.8 %all-gather.3 = f32[4,9,1024]{2,1,0:T(8,128)S(1)} all-gather(f32[1,9,1024]{2,1,0:T(8,128)S(1)} %maximum_bitcast_fusion.1), channel_id=3, replica_groups=mesh['level'=4,'body'=8] {'level'}, dimensions={0}, use_global_device_ids=true | all-gather | bytes 184320 | tf_op jit(solution)/shard_map/all_gather | solution.py:207
  94.2 0.1 fusion.11
  94.4 0.6 copy.11
  (17 shorter events, 0.3 us)
Async XLA Ops:
  0.0 0.7 copy-start.1
  1.4 6.2 %copy-start = (f32[1,3,6,1024]{3,0,2,1:T(1,128)S(1)}, f32[1,3,6,1024]{3,0,2,1:T(1,128)}, u32[]{:S(2)}) copy-start(f32[1,3,6,1024]{3,0,2,1:T(1,128)} %param.4) | copy-start | bytes 221188
  8.5 15.8 %all-to-all-start = ((f32[8,8,1024]{2,1,0:T(8,128)}), f32[8,8,1024]{2,1,0:T(8,128)S(1)}, u32[]{:S(2)}, u32[]{:S(2)}) async-start(f32[8,8,1024]{2,1,0:T(8,128)} %broadcast_in_dim.39), calls=%async_computation | async-start | bytes 524288 | tf_op jit(solution)/shard_map/all_to_all | solution.py:161
